TPU v7x, 32 devices: a whole 2x2x4 slice. The times are simulated.
32 devices in a mesh: tm: 8 (over z, y), row: 2 (over core), col: 2 (over x).
Axes of the slice: x: 2, y: 2, z: 4, core: 2. Of those that a mesh axis runs over, the one named last changes fastest.
Arguments:
- precision_diag: float32 [16, 512, 512], P('tm', 'row', 'col'), may hold values from -4 to 16
- precision_link: float32 [16, 512, 512], P('tm', 'row', 'col'), may hold values from -8 to 2
Outputs:
- pivots: float32 [16, 512, 512], P('tm', 'row', 'col')
- couplings: float32 [16, 512, 512], P('tm', 'row', 'col')
- log_variance: float32 [16, 512], P('tm', ('row', 'col'))
All inputs are finite; a program needn't handle non-finite values.
Results may differ from a plain program's by a relative error of at most 0.0003.
Values sent between devices are 32-bit elements; how exact they have to be, the bound alone decides.
A program may use at most 128 MiB of HBM per device.

v0:
```python
import jax
import jax.numpy as jnp
from jax import lax
from jax.sharding import PartitionSpec as P

LEVELS = 4


def shifted(array, axis, by):
    devices = lax.axis_size(axis)
    pairs = [(i, i + by) for i in range(devices) if 0 <= i + by < devices]
    return lax.ppermute(array, axis, pairs)


def product_tn(left_part, right_part):
    return jnp.einsum("ki,kl->il", left_part, right_part, precision=lax.Precision.HIGHEST)


def factor_solve(pivot, right_side):
    lower_factor = jnp.linalg.cholesky(pivot)
    return jax.scipy.linalg.solve_triangular(lower_factor, right_side, lower=True)


def unit_columns(node_count, diag_id):
    quarter = node_count // 4
    row_positions = jnp.arange(node_count)[:, None]
    col_positions = diag_id * quarter + jnp.arange(quarter)[None, :]
    return (row_positions == col_positions).astype(jnp.float32)


def log_variance(inverse_cols):
    return jnp.log(jnp.sum(inverse_cols * inverse_cols, axis=0))


def column_half(panel, index_id):
    half_width = panel.shape[1] // 2
    return lax.dynamic_slice_in_dim(panel, index_id * half_width, half_width, 1)


def whole_blocks(stacked):
    widened = lax.all_gather(stacked, "col", axis=2, tiled=True)
    return lax.all_gather(widened, "row", axis=1, tiled=True)


def send_later(gram_up, link_new, stride):
    return shifted((gram_up, link_new), "tm", stride)


def guarded(active, compute, zero_fill, operands):
    if active is None:
        return compute(operands)
    return lax.cond(active, compute, zero_fill, operands)


def solve_divided(operands, place):
    row_id, col_id, diag_id = place
    pivot, below_cols, above_rows = operands
    node_count = pivot.shape[0]
    half_width = below_cols.shape[1]
    right_side = jnp.concatenate(
        [below_cols, above_rows.T, unit_columns(node_count, diag_id)], axis=1
    )
    solved = factor_solve(pivot, right_side)
    lower_own = solved[:, :half_width]
    upper_own = solved[:, half_width : 2 * half_width]
    log_part = log_variance(solved[:, 2 * half_width :])
    return (log_part, lower_own, upper_own, -product_tn(upper_own, lower_own))


def gram_divided(panels, place):
    row_id, col_id, diag_id = place
    lower_whole, upper_whole = panels
    return (
        product_tn(column_half(lower_whole, row_id), column_half(lower_whole, col_id)),
        product_tn(column_half(upper_whole, row_id), column_half(upper_whole, col_id)),
    )


def eliminate(pivot_tile, below_tile, above_tile, active, place):
    half_width = pivot_tile.shape[0]
    node_count = 2 * half_width
    log_zero = jnp.zeros((node_count // 4,), jnp.float32)
    tile_zero = jnp.zeros((half_width, half_width), jnp.float32)
    pivot = whole_blocks(pivot_tile[None])[0]
    below_cols = lax.all_gather(below_tile, "row", axis=0, tiled=True)
    above_rows = lax.all_gather(above_tile, "col", axis=1, tiled=True)
    panel_zero = jnp.zeros((node_count, half_width), jnp.float32)
    log_part, lower_own, upper_own, link_new = guarded(
        active,
        lambda operands: solve_divided(operands, place),
        lambda operands: (log_zero, panel_zero, panel_zero, tile_zero),
        (pivot, below_cols, above_rows),
    )
    lower_whole = lax.all_gather(lower_own, "col", axis=1, tiled=True)
    upper_whole = lax.all_gather(upper_own, "row", axis=1, tiled=True)
    gram_down, gram_up = guarded(
        active,
        lambda operands: gram_divided(operands, place),
        lambda operands: (tile_zero, tile_zero),
        (lower_whole, upper_whole),
    )
    return (log_part, gram_down, gram_up, link_new)


def final_log(pivot, place):
    row_id, col_id, diag_id = place
    inverse_cols = factor_solve(pivot, unit_columns(pivot.shape[0], diag_id))
    return log_variance(inverse_cols)


def shards(precision_diag, precision_link):
    row_id = lax.axis_index("row")
    col_id = lax.axis_index("col")
    time_id = lax.axis_index("tm")
    place = (row_id, col_id, row_id * 2 + col_id)
    device_count = lax.axis_size("tm")
    pivot_low = precision_diag[0]
    pivot_high = precision_diag[1]
    link_low = precision_link[0]
    link_high = jnp.where(
        time_id == device_count - 1, jnp.zeros_like(precision_link[1]), precision_link[1]
    )
    log_high, gram_down, gram_up, link_low = eliminate(pivot_high, link_low, link_high, None, place)
    ahead_gram, from_below = send_later(gram_up, link_low, 1)
    pivot_low = pivot_low - gram_down - ahead_gram
    log_low = jnp.zeros_like(log_high)
    for level_num in range(1, LEVELS):
        stride = 2 ** (level_num - 1)
        position = time_id % (2 * stride)
        active = position == stride
        keeper = position == 0
        below_link = from_below
        log_now, gram_down, gram_up, link_new = eliminate(
            pivot_low, below_link, link_low, active, place
        )
        back_gram, back_link = shifted((gram_down, link_new), "tm", -stride)
        ahead_gram, from_below = send_later(gram_up, link_new, stride)
        log_low = jnp.where(active, log_now, log_low)
        pivot_low = pivot_low - back_gram - ahead_gram
        link_low = jnp.where(keeper, back_link, link_low)
    remaining = time_id % 2 ** (LEVELS - 1) == 0
    whole_pivot = whole_blocks(pivot_low[None])[0]
    log_final = lax.cond(
        remaining,
        lambda pivot: final_log(pivot, place),
        lambda pivot: jnp.zeros_like(log_low),
        whole_pivot,
    )
    log_low = jnp.where(remaining, log_final, log_low)
    pivots = jnp.stack([pivot_low, pivot_high])
    couplings = jnp.stack([link_low, link_high])
    logs = jnp.stack([log_low, log_high])
    return (pivots, couplings, logs)


def solution(mesh):
    in_specs = (P("tm", "row", "col"), P("tm", "row", "col"))
    out_specs = (P("tm", "row", "col"), P("tm", "row", "col"), P("tm", ("row", "col")))
    return jax.shard_map(shards, mesh=mesh, in_specs=in_specs, out_specs=out_specs, check_vma=False)
```

profile of v0, /device:TPU:0, one launch (start us, length us, event | category | flops | bytes accessed | tf_op | source)
XLA Modules:
  0.0 1136.3 jit_solution(9765226666093898980)
XLA Ops:
  9.2 10.0 all_gather.78
  21.7 9.0 all-gather.1
  36.1 11.7 %cholesky.838 = f32[128,128]{1,0:T(8,128)S(1)} custom-call(f32[128,128]{1,0:T(8,128)S(1)} %cholesky.958), custom_call_target="Cholesky" | custom-call | tf_op jit(solution)/shard_map/jit(cholesky)/cholesky | solution.py:20
  47.8 9.8 custom-call.57
  60.3 11.7 %cholesky.857 = f32[128,128]{1,0:T(8,128)S(1)} custom-call(f32[128,128]{1,0:T(8,128)S(1)} %cholesky.962), custom_call_target="Cholesky" | custom-call | tf_op jit(solution)/shard_map/jit(cholesky)/cholesky | solution.py:20
  72.1 10.1 custom-call.58
  83.8 11.7 %cholesky.878 = f32[128,128]{1,0:T(8,128)S(1)} custom-call(f32[128,128]{1,0:T(8,128)S(1)} %cholesky.967), custom_call_target="Cholesky" | custom-call | tf_op jit(solution)/shard_map/jit(cholesky)/cholesky | solution.py:20
  96.2 9.8 custom-call.59
  107.5 11.7 %cholesky.895 = f32[128,128]{1,0:T(8,128)S(1)} custom-call(f32[128,128]{1,0:T(8,128)S(1)} %convolution_subtract_fusion.30), custom_call_target="Cholesky" | custom-call | tf_op jit(solution)/shard_map/jit(cholesky)/cholesky | solution.py:20
  124.5 11.6 %while.13 = (s32[]{:T(128)}, f32[512,512]{1,0:T(8,128)}, s32[4,2]{0,1:T(2,128)S(1)}, f32[4,128,128]{2,1,0:T(8,128)S(1)}, s32[]{:T(128)}) while((s32[]{:T(128)}, f32[512,512]{1,0:T(8,128)}, s32[4,2]{0,1:T(2,128)S(1)}, f32[4,128,128]{2,1,0:T(8,128)S(1)}, s32[]{:T(128)}) %tuple.211), condition=%wide.while_cond.clone.2, body=%wide.while_body.clone.2.sunk | while | flops 2 | bytes 131189 | solution.py:21
  136.1 39.3 %custom-call.60 = f32[4,128,128]{1,2,0:T(8,128)S(1)} custom-call(f32[4,128,128]{2,1,0:T(8,128)S(1)} %get-tuple-element.163), custom_call_target="InvertDiagBlocksLowerTriangular" | custom-call | tf_op jit(solution)/shard_map/jit(_solve_triangular)/triangular_solve | solution.py:21
  185.9 9.9 all-gather.28.cloned.1.call-done
  201.9 18.5 %all-gather.26.cloned.1.call-done = f32[512,512]{1,0:T(8,128)} async-done(((f32[512,256]{1,0:T(8,128)}), f32[512,512]{1,0:T(8,128)}) %all-gather.26.cloned.1.call-update) | async-done | bytes 1048592 | tf_op jit(solution)/shard_map/all_gather | solution.py:94
  222.7 8.6 all-gather.2
  235.8 7.3 all_gather.86
  245.3 5.0 conditional.7
  251.0 184.8 %all-gather.30.cloned.1.call-done = f32[512,512]{1,0:T(8,128)} async-done(((f32[512,256]{1,0:T(8,128)}), f32[512,512]{1,0:T(8,128)}) %all-gather.30.cloned.1.call-update) | async-done | bytes 1048592 | tf_op jit(solution)/shard_map/all_gather | solution.py:94
  435.8 11.0 all-gather.32.cloned.1.call-done
  447.2 7.1 collective-permute-start.3
  455.6 10.3 collective-permute-done.3
  466.0 8.4 all-gather.4
  476.0 5.0 collective-permute-start.5
  484.0 7.0 all_gather.92
  493.4 4.8 conditional.9
  499.0 192.1 %all-gather.34.cloned.1.call-done = f32[512,512]{1,0:T(8,128)} async-done(((f32[512,256]{1,0:T(8,128)}), f32[512,512]{1,0:T(8,128)}) %all-gather.34.cloned.1.call-update) | async-done | bytes 1048592 | tf_op jit(solution)/shard_map/all_gather | solution.py:94
  691.1 11.2 all-gather.36.cloned.1.call-done
  702.6 7.1 collective-permute-start.7
  711.0 4.7 collective-permute-done.7
  720.6 8.1 all-gather.6
  737.4 7.0 all_gather.98
  746.7 5.0 conditional.11
  752.4 184.5 %all-gather.38.cloned.1.call-done = f32[512,512]{1,0:T(8,128)} async-done(((f32[512,256]{1,0:T(8,128)}), f32[512,512]{1,0:T(8,128)}) %all-gather.38.cloned.1.call-update) | async-done | bytes 1048592 | tf_op jit(solution)/shard_map/all_gather | solution.py:94
  936.9 11.0 all-gather.40.cloned.1.call-done
  948.3 8.0 collective-permute-start.11
  957.6 4.8 collective-permute-done.11
  962.4 8.2 collective-permute-done.10
  970.7 9.1 all-gather.8
  981.4 8.7 collective-permute-done.12
  992.0 136.6 %conditional.13 = (f32[128]{0:T(128)S(1)}) conditional(s32[]{:T(128)} %convert_element_type.34, () %tuple.76, (f32[1,512,512]{1,2,0:T(8,128)}, s32[]{:T(128)}) %tuple.257), branch_computations={%region_23.26_spmd, %region_24.28_spmd} | conditional | flops 656916992 | bytes 27548512 | solution.py:143
  995.2 11.7 %cholesky.766 = f32[128,128]{1,0:T(8,128)S(1)} custom-call(f32[128,128]{1,0:T(8,128)S(1)} %cholesky.919), custom_call_target="Cholesky" | custom-call | tf_op jit(solution)/shard_map/cond/branch_1_fun/jit(cholesky)/cholesky | solution.py:20
  1006.9 9.8 custom-call.54
  1017.6 11.7 %cholesky.785 = f32[128,128]{1,0:T(8,128)S(1)} custom-call(f32[128,128]{1,0:T(8,128)S(1)} %cholesky.923), custom_call_target="Cholesky" | custom-call | tf_op jit(solution)/shard_map/cond/branch_1_fun/jit(cholesky)/cholesky | solution.py:20
  1031.3 10.0 custom-call.55
  1042.0 11.7 %cholesky.806 = f32[128,128]{1,0:T(8,128)S(1)} custom-call(f32[128,128]{1,0:T(8,128)S(1)} %cholesky.928), custom_call_target="Cholesky" | custom-call | tf_op jit(solution)/shard_map/cond/branch_1_fun/jit(cholesky)/cholesky | solution.py:20
  1055.0 9.8 custom-call.56
  1065.4 11.7 %cholesky.823 = f32[128,128]{1,0:T(8,128)S(1)} custom-call(f32[128,128]{1,0:T(8,128)S(1)} %convolution_subtract_fusion.11), custom_call_target="Cholesky" | custom-call | tf_op jit(solution)/shard_map/cond/branch_1_fun/jit(cholesky)/cholesky | solution.py:20
  1078.9 8.1 while.12
  1087.0 39.3 %custom-call.26 = f32[4,128,128]{1,2,0:T(8,128)S(1)} custom-call(f32[4,128,128]{2,1,0:T(8,128)S(1)} %get-tuple-element.141), custom_call_target="InvertDiagBlocksLowerTriangular" | custom-call | tf_op jit(solution)/shard_map/cond/branch_1_fun/jit(_solve_triangular)/triangular_solve | solution.py:21
  (253 shorter events, 111.6 us)
Async XLA Ops:
  7.2 12.1 %copy-start.38 = (f32[2,256,256]{2,1,0:T(8,128)S(1)}, f32[2,256,256]{2,1,0:T(8,128)}, u32[]{:S(2)}) copy-start(f32[2,256,256]{2,1,0:T(8,128)} %param.20) | copy-start | bytes 1572868
  7.2 23.8 %all-gather.24.cloned.1.call-start = ((), (), s32[]{:S(2)}) async-start(), calls=%async_computation | async-start | bytes 1572864 | tf_op jit(solution)/shard_map/all_gather | solution.py:42
  9.2 10.3 copy-start.17
  19.2 176.6 %all-gather.28.cloned.1.call-start = ((), (), s32[]{:S(2)}) async-start(), calls=%async_computation.2 | async-start | bytes 1572864 | tf_op jit(solution)/shard_map/all_gather | solution.py:95
  19.4 11.6 %copy-start.19 = (f32[1,256,256]{2,1,0:T(8,128)}, f32[1,256,256]{2,1,0:T(8,128)S(1)}, u32[]{:S(2)}) copy-start(f32[1,256,256]{2,1,0:T(8,128)S(1)} %get-tuple-element.290) | copy-start | bytes 786436
  185.1 16.7 %copy-start.37 = (f32[1,256,256]{2,1,0:T(8,128)S(1)}, f32[1,256,256]{2,1,0:T(8,128)}, u32[]{:S(2)}) copy-start(f32[1,256,256]{2,1,0:T(8,128)} %get-tuple-element.287) | copy-start | bytes 786436
  185.1 35.3 %all-gather.26.cloned.1.call-start = ((), (), s32[]{:S(2)}) async-start(), calls=%async_computation.1 | async-start | bytes 1572864 | tf_op jit(solution)/shard_map/all_gather | solution.py:94
  185.8 59.5 %all-gather.42.cloned.1.call-start = ((), (), s32[]{:S(2)}) async-start(), calls=%async_computation.9 | async-start | bytes 1572864 | tf_op jit(solution)/shard_map/all_gather | solution.py:42
  198.1 22.3 %collective-permute-start = (f32[256,256]{0,1:T(8,128)S(1)}, f32[256,256]{0,1:T(8,128)S(1)}, u32[]{:S(2)}, u32[]{:S(2)}) collective-permute-start(f32[256,256]{0,1:T(8,128)S(1)} %fusion.162), channel_id=1, source_target_pairs={{0,4},{4,8},{8,12},{12,16},{16,20},{20,24},{24,28},{1,5},{5,9},{9,... | collective-permute-start | bytes 786440 | tf_op jit(solution)/shard_map/ppermute | solution.py:12
  231.3 204.5 %all-gather.30.cloned.1.call-start = ((), (), s32[]{:S(2)}) async-start(), calls=%async_computation.3 | async-start | bytes 1572864 | tf_op jit(solution)/shard_map/all_gather | solution.py:94
  232.4 12.9 %copy-start.13 = (f32[256,256]{1,0:T(8,128)}, f32[256,256]{1,0:T(8,128)S(1)}, u32[]{:S(2)}) copy-start(f32[256,256]{1,0:T(8,128)S(1)} %convolution_negate_fusion.3) | copy-start | bytes 786436
  232.4 10.7 collective-permute-start.1
  250.4 196.5 %all-gather.32.cloned.1.call-start = ((), (), s32[]{:S(2)}) async-start(), calls=%async_computation.4 | async-start | bytes 1572864 | tf_op jit(solution)/shard_map/all_gather | solution.py:95
  250.9 242.4 %all-gather.44.cloned.1.call-start = ((), (), s32[]{:S(2)}) async-start(), calls=%async_computation.10 | async-start | bytes 1572864 | tf_op jit(solution)/shard_map/all_gather | solution.py:42
  446.9 19.1 %copy-start.16 = (f32[256,256]{0,1:T(8,128)S(1)}, f32[256,256]{0,1:T(8,128)}, u32[]{:S(2)}) copy-start(f32[256,256]{0,1:T(8,128)} %copy-done.15) | copy-start | bytes 786436
  447.2 36.8 %copy-start.14 = (f32[256,256]{1,0:T(8,128)S(1)}, f32[256,256]{1,0:T(8,128)}, u32[]{:S(2)}) copy-start(f32[256,256]{1,0:T(8,128)} %copy-done.13) | copy-start | bytes 786436
  447.2 18.7 %collective-permute-start.3 = (f32[256,256]{0,1:T(8,128)S(1)}, f32[256,256]{0,1:T(8,128)S(1)}, u32[]{:S(2)}, u32[]{:S(2)}) collective-permute-start(f32[256,256]{0,1:T(8,128)S(1)} %copy.17), channel_id=1, source_target_pairs={{0,4},{4,8},{8,12},{12,16},{16,20},{20,24},{24,28},{1,5},{5,9},{9,... | collective-permute-start | bytes 786440 | tf_op jit(solution)/shard_map/ppermute | solution.py:12
  454.3 11.6 %collective-permute-start.2 = (f32[256,256]{0,1:T(8,128)S(1)}, f32[256,256]{0,1:T(8,128)S(1)}, u32[]{:S(2)}, u32[]{:S(2)}) collective-permute-start(f32[256,256]{0,1:T(8,128)S(1)} %copy.16), channel_id=1, source_target_pairs={{4,0},{8,4},{12,8},{16,12},{20,16},{24,20},{28,24},{5,1},{9,5},{13... | collective-permute-start | bytes 786440 | tf_op jit(solution)/shard_map/ppermute | solution.py:12
  466.0 18.0 %copy-start.25 = (f32[256,256]{0,1:T(8,128)}, f32[256,256]{0,1:T(8,128)S(1)}, u32[]{:S(2)}) copy-start(f32[256,256]{0,1:T(8,128)S(1)} %subtract_subtract_fusion.2) | copy-start | bytes 786436
  474.5 216.6 %all-gather.34.cloned.1.call-start = ((), (), s32[]{:S(2)}) async-start(), calls=%async_computation.5 | async-start | bytes 1572864 | tf_op jit(solution)/shard_map/all_gather | solution.py:94
  474.5 9.4 collective-permute-start.4
  476.0 15.1 %collective-permute-start.5 = (f32[256,256]{0,1:T(8,128)S(1)}, f32[256,256]{0,1:T(8,128)S(1)}, u32[]{:S(2)}, u32[]{:S(2)}) collective-permute-start(f32[256,256]{0,1:T(8,128)S(1)} %copy.18), channel_id=1, source_target_pairs={{0,4},{4,8},{8,12},{12,16},{16,20},{20,24},{24,28},{1,5},{5,9},{9,... | collective-permute-start | bytes 786440 | tf_op jit(solution)/shard_map/ppermute | solution.py:12
  484.0 9.4 copy-start.23
  498.2 204.1 %copy-start.35 = (f32[256,256]{1,0:T(8,128)}, f32[256,256]{1,0:T(8,128)S(1)}, u32[]{:S(2)}) copy-start(f32[256,256]{1,0:T(8,128)S(1)} %get-tuple-element.117) | copy-start | bytes 786436
  498.3 204.0 %all-gather.36.cloned.1.call-start = ((), (), s32[]{:S(2)}) async-start(), calls=%async_computation.6 | async-start | bytes 1572864 | tf_op jit(solution)/shard_map/all_gather | solution.py:95
  499.0 247.7 %all-gather.46.cloned.1.call-start = ((), (), s32[]{:S(2)}) async-start(), calls=%async_computation.11 | async-start | bytes 1572864 | tf_op jit(solution)/shard_map/all_gather | solution.py:42
  702.3 17.6 %copy-start.26 = (f32[256,256]{0,1:T(8,128)S(1)}, f32[256,256]{0,1:T(8,128)}, u32[]{:S(2)}) copy-start(f32[256,256]{0,1:T(8,128)} %copy-done.25) | copy-start | bytes 786436
  702.6 26.2 %copy-start.36 = (f32[256,256]{1,0:T(8,128)S(1)}, f32[256,256]{1,0:T(8,128)}, u32[]{:S(2)}) copy-start(f32[256,256]{1,0:T(8,128)} %copy-done.35) | copy-start | bytes 786436
  702.6 34.7 %copy-start.24 = (f32[256,256]{1,0:T(8,128)S(1)}, f32[256,256]{1,0:T(8,128)}, u32[]{:S(2)}) copy-start(f32[256,256]{1,0:T(8,128)} %copy-done.23) | copy-start | bytes 786436
  702.6 13.1 %collective-permute-start.7 = (f32[256,256]{0,1:T(8,128)S(1)}, f32[256,256]{0,1:T(8,128)S(1)}, u32[]{:S(2)}, u32[]{:S(2)}) collective-permute-start(f32[256,256]{0,1:T(8,128)S(1)} %copy.20), channel_id=1, source_target_pairs={{0,8},{4,12},{8,16},{12,20},{16,24},{20,28},{1,9},{5,13},{9,17},{1... | collective-permute-start | bytes 786440 | tf_op jit(solution)/shard_map/ppermute | solution.py:12
  709.7 10.1 collective-permute-start.6
  728.8 208.1 %all-gather.38.cloned.1.call-start = ((), (), s32[]{:S(2)}) async-start(), calls=%async_computation.7 | async-start | bytes 1572864 | tf_op jit(solution)/shard_map/all_gather | solution.py:94
  728.9 8.5 collective-permute-start.8
  730.3 14.1 %collective-permute-start.9 = (f32[256,256]{0,1:T(8,128)S(1)}, f32[256,256]{0,1:T(8,128)S(1)}, u32[]{:S(2)}, u32[]{:S(2)}) collective-permute-start(f32[256,256]{0,1:T(8,128)S(1)} %copy.21), channel_id=1, source_target_pairs={{0,8},{4,12},{8,16},{12,20},{16,24},{20,28},{1,9},{5,13},{9,17},{1... | collective-permute-start | bytes 786440 | tf_op jit(solution)/shard_map/ppermute | solution.py:12
  737.4 9.4 copy-start.27
  751.7 196.2 %copy-start.39 = (f32[256,256]{1,0:T(8,128)}, f32[256,256]{1,0:T(8,128)S(1)}, u32[]{:S(2)}) copy-start(f32[256,256]{1,0:T(8,128)S(1)} %get-tuple-element.122) | copy-start | bytes 786436
  751.7 196.2 %all-gather.40.cloned.1.call-start = ((), (), s32[]{:S(2)}) async-start(), calls=%async_computation.8 | async-start | bytes 1572864 | tf_op jit(solution)/shard_map/all_gather | solution.py:95
  752.3 239.7 %all-gather.48.cloned.1.call-start = ((), (), s32[]{:S(2)}) async-start(), calls=%async_computation.12 | async-start | bytes 1572864 | tf_op jit(solution)/shard_map/all_gather | solution.py:42
  947.9 22.6 %copy-start.22 = (f32[256,256]{0,1:T(8,128)S(1)}, f32[256,256]{0,1:T(8,128)}, u32[]{:S(2)}) copy-start(f32[256,256]{0,1:T(8,128)} %copy-done.21) | copy-start | bytes 786436
  948.3 31.5 %copy-start.40 = (f32[256,256]{1,0:T(8,128)S(1)}, f32[256,256]{1,0:T(8,128)}, u32[]{:S(2)}) copy-start(f32[256,256]{1,0:T(8,128)} %copy-done.39) | copy-start | bytes 786436
  948.3 33.0 %copy-start.1 = (f32[128,640]{1,0:T(8,128)S(1)}, f32[128,640]{1,0:T(8,128)}, u32[]{:S(2)}) copy-start(f32[128,640]{1,0:T(8,128)} %copy-done) | copy-start | bytes 983044
  948.3 14.1 %collective-permute-start.11 = (f32[256,256]{0,1:T(8,128)S(1)}, f32[256,256]{0,1:T(8,128)S(1)}, u32[]{:S(2)}, u32[]{:S(2)}) collective-permute-start(f32[256,256]{0,1:T(8,128)S(1)} %copy.23), channel_id=1, source_target_pairs={{0,16},{4,20},{8,24},{12,28},{1,17},{5,21},{9,25},{13,29},{2,18},{... | collective-permute-start | bytes 786440 | tf_op jit(solution)/shard_map/ppermute | solution.py:12
  956.3 14.3 %collective-permute-start.10 = (f32[256,256]{0,1:T(8,128)S(1)}, f32[256,256]{0,1:T(8,128)S(1)}, u32[]{:S(2)}, u32[]{:S(2)}) collective-permute-start(f32[256,256]{0,1:T(8,128)S(1)} %copy.22), channel_id=1, source_target_pairs={{16,0},{20,4},{24,8},{28,12},{17,1},{21,5},{25,9},{29,13},{18,2},{... | collective-permute-start | bytes 786440 | tf_op jit(solution)/shard_map/ppermute | solution.py:12
  970.6 19.5 %copy-start.28 = (f32[256,256]{1,0:T(8,128)S(1)}, f32[256,256]{1,0:T(8,128)}, u32[]{:S(2)}) copy-start(f32[256,256]{1,0:T(8,128)} %copy-done.27) | copy-start | bytes 786436
  979.8 10.4 copy-start.20
  979.8 10.3 collective-permute-start.12
  981.3 9.7 copy-start.18
  995.2 21.7 %copy-start.11 = (f32[512,512]{1,0:T(8,128)S(1)}, f32[512,512]{1,0:T(8,128)}, u32[]{:S(2)}) copy-start(f32[512,512]{1,0:T(8,128)} %copy-done.10) | copy-start | bytes 3145732 | tf_op jit(solution)/shard_map/cond
  (7 other events, 19.1 us)
Sparse Core Ops, SparseCore 0:
  19.4 10.5 all-gather.23
  185.2 10.5 all-gather.27
  197.9 22.4 all-gather.25
  231.4 9.0 all-gather.41
  250.5 185.3 all-gather.29
  437.8 9.0 all-gather.31
  474.6 10.2 all-gather.43
  498.4 192.6 all-gather.33
  693.2 9.0 all-gather.35
  728.9 8.0 all-gather.45
  751.9 184.9 all-gather.37
  938.9 9.0 all-gather.39
  979.9 6.2 all-gather.47
where the time goes:
time: 1150 us; the launch traced here: 1140 us
  waiting for transfers between devices  672 us (58%)
  other arithmetic  242 us (21%)
  blocking collectives  83.7 us (7%)
  starting transfers between devices  47.2 us (4%)
  local copies, waits for them, and re-layouts  37.3 us (3%)
  matrix products  23.3 us (2%)
  between operations  18.1 us (2%)
  loops' own time  13.3 us (1%)
    all_gather x4, waiting for transfers between devices, eliminate(): lower_whole = lax.all_gather(lower_own, 'col', axis=1, tiled=True)  580 us
    another operation x28, other arithmetic, factor_solve(): lower_factor = jnp.linalg.cholesky(pivot)  157 us
    another operation x8, other arithmetic, factor_solve(): jax.scipy.linalg.solve_triangular(lower_factor, right_side, lower=True)  80.2 us
    ppermute x13, starting transfers between devices, shifted(): return lax.ppermute(array, axis, pairs)  46.7 us
    ppermute x13, waiting for transfers between devices, shifted(): return lax.ppermute(array, axis, pairs)  46.3 us
    all_gather x5, blocking collectives, whole_blocks(): widened = lax.all_gather(stacked, 'col', axis=2, tiled=True)  44.3 us
    all_gather x4, waiting for transfers between devices, eliminate(): upper_whole = lax.all_gather(upper_own, 'row', axis=1, tiled=True)  43.2 us
    all_gather x4, blocking collectives, eliminate(): above_rows = lax.all_gather(above_tile, 'col', axis=1, tiled=True)  30.4 us
  transfers between devices with their start and end apart: 26, of which 16 were waited for; matrix products, arithmetic and copies ran while one was open for 1% of the time, Pallas kernels for 0%

commit v1 on v0

--- a/solution.py
+++ b/solution.py
@@ -91,7 +91,10 @@
         lambda operands: (log_zero, panel_zero, panel_zero, tile_zero),
         (pivot, below_cols, above_rows),
     )
-    lower_whole = lax.all_gather(lower_own, "col", axis=1, tiled=True)
+    count = lax.axis_size("col")
+    blocks = jnp.stack([lower_own for _ in range(count)])
+    blocks = lax.all_to_all(blocks, "col", split_axis=0, concat_axis=0)
+    lower_whole = jnp.concatenate(blocks, axis=1)
     upper_whole = lax.all_gather(upper_own, "row", axis=1, tiled=True)
     gram_down, gram_up = guarded(
         active,

time: 1150 us -> 1090 us (0.948)
  waiting for transfers between devices: 672 us -> 557 us
  starting transfers between devices: 47.2 us -> 96.9 us
    all_gather x4 -> x0, waiting for transfers between devices: 580 us -> none  [eliminate(): lower_whole = lax.all_gather(lower_own, 'col', axis=1, tiled=True)]
    all_gather x4, waiting for transfers between devices: 43.2 us -> 468 us  [eliminate(): upper_whole = lax.all_gather(upper_own, 'row', axis=1, tiled=True)]
    all_to_all x0 -> x4, waiting for transfers between devices: none -> 42.3 us  [eliminate(): blocks = lax.all_to_all(blocks, 'col', split_axis=0, concat_axis=0)]
    ppermute x13, starting transfers between devices: 46.7 us -> 82.2 us  [shifted(): return lax.ppermute(array, axis, pairs)]
    all_to_all x0 -> x4, starting transfers between devices: none -> 14.3 us  [eliminate(): blocks = lax.all_to_all(blocks, 'col', split_axis=0, concat_axis=0)]
  transfers between devices with their start and end apart: 26 -> 26, of which waited for: 16 -> 16; matrix products, arithmetic and copies ran while one was open for 1% -> 2% of each run, Pallas kernels for 0% -> 0%
where the time goes in v1:
time: 1090 us; the launch traced here: 1080 us
  waiting for transfers between devices  557 us (51%)
  other arithmetic  249 us (23%)
  starting transfers between devices  96.9 us (9%)
  blocking collectives  79.6 us (7%)
  local copies, waits for them, and re-layouts  40.8 us (4%)
  matrix products  21.7 us (2%)
  between operations  17.8 us (2%)
  loops' own time  13.7 us (1%)
    all_gather x4, waiting for transfers between devices, eliminate(): upper_whole = lax.all_gather(upper_own, 'row', axis=1, tiled=True)  468 us
    another operation x28, other arithmetic, factor_solve(): lower_factor = jnp.linalg.cholesky(pivot)  157 us
    ppermute x13, starting transfers between devices, shifted(): return lax.ppermute(array, axis, pairs)  82.2 us
    another operation x8, other arithmetic, factor_solve(): jax.scipy.linalg.solve_triangular(lower_factor, right_side, lower=True)  80.2 us
    ppermute x13, waiting for transfers between devices, shifted(): return lax.ppermute(array, axis, pairs)  46.4 us
    all_to_all x4, waiting for transfers between devices, eliminate(): blocks = lax.all_to_all(blocks, 'col', split_axis=0, concat_axis=0)  42.3 us
    all_gather x5, blocking collectives, whole_blocks(): widened = lax.all_gather(stacked, 'col', axis=2, tiled=True)  40.2 us
    all_gather x4, blocking collectives, eliminate(): above_rows = lax.all_gather(above_tile, 'col', axis=1, tiled=True)  30.4 us
  transfers between devices with their start and end apart: 26, of which 16 were waited for; matrix products, arithmetic and copies ran while one was open for 2% of the time, Pallas kernels for 0%

profile of v1, /device:TPU:0, one launch (start us, length us, event | category | flops | bytes accessed | tf_op | source)
XLA Modules:
  0.0 1075.9 jit_solution(9866799419962216669)
XLA Ops:
  9.2 10.0 all_gather.66
  21.8 9.0 all-gather.1
  36.0 11.7 %cholesky.838 = f32[128,128]{1,0:T(8,128)S(1)} custom-call(f32[128,128]{1,0:T(8,128)S(1)} %cholesky.958), custom_call_target="Cholesky" | custom-call | tf_op jit(solution)/shard_map/jit(cholesky)/cholesky | solution.py:20
  47.8 9.8 custom-call.57
  60.3 11.7 %cholesky.857 = f32[128,128]{1,0:T(8,128)S(1)} custom-call(f32[128,128]{1,0:T(8,128)S(1)} %cholesky.962), custom_call_target="Cholesky" | custom-call | tf_op jit(solution)/shard_map/jit(cholesky)/cholesky | solution.py:20
  72.0 10.0 custom-call.58
  83.5 11.7 %cholesky.878 = f32[128,128]{1,0:T(8,128)S(1)} custom-call(f32[128,128]{1,0:T(8,128)S(1)} %cholesky.967), custom_call_target="Cholesky" | custom-call | tf_op jit(solution)/shard_map/jit(cholesky)/cholesky | solution.py:20
  95.9 9.8 custom-call.59
  107.2 11.7 %cholesky.895 = f32[128,128]{1,0:T(8,128)S(1)} custom-call(f32[128,128]{1,0:T(8,128)S(1)} %convolution_subtract_fusion.30), custom_call_target="Cholesky" | custom-call | tf_op jit(solution)/shard_map/jit(cholesky)/cholesky | solution.py:20
  124.2 11.2 %while.13 = (s32[]{:T(128)}, f32[512,512]{1,0:T(8,128)}, s32[4,2]{0,1:T(2,128)S(1)}, f32[4,128,128]{2,1,0:T(8,128)S(1)}, s32[]{:T(128)}) while((s32[]{:T(128)}, f32[512,512]{1,0:T(8,128)}, s32[4,2]{0,1:T(2,128)S(1)}, f32[4,128,128]{2,1,0:T(8,128)S(1)}, s32[]{:T(128)}) %tuple.218), condition=%wide.while_cond.clone.2, body=%wide.while_body.clone.2.sunk | while | flops 2 | bytes 131189 | solution.py:21
  135.4 39.3 %custom-call.60 = f32[4,128,128]{1,2,0:T(8,128)S(1)} custom-call(f32[4,128,128]{2,1,0:T(8,128)S(1)} %get-tuple-element.166), custom_call_target="InvertDiagBlocksLowerTriangular" | custom-call | tf_op jit(solution)/shard_map/jit(_solve_triangular)/triangular_solve | solution.py:21
  186.9 6.0 all-gather.22.cloned.1.call-done
  196.0 4.3 collective-permute-start
  207.8 8.4 all-gather.2
  217.3 4.4 collective-permute-start.1
  221.7 7.3 all_gather.73
  231.3 5.1 conditional.7
  242.3 14.1 %all-to-all-done.1 = f32[2,512,256]{2,1,0:T(8,128)S(1)} async-done(((f32[2,512,256]{2,1,0:T(8,128)}), f32[2,512,256]{2,1,0:T(8,128)S(1)}, u32[]{:S(2)}, u32[]{:S(2)}) %all-to-all-start.1) | async-done | bytes 1048608 | tf_op jit(solution)/shard_map/all_to_all | solution.py:96
  256.5 152.6 %all-gather.24.cloned.1.call-done = f32[512,512]{1,0:T(8,128)} async-done(((f32[512,256]{1,0:T(8,128)}), f32[512,512]{1,0:T(8,128)}) %all-gather.24.cloned.1.call-update) | async-done | bytes 1048592 | tf_op jit(solution)/shard_map/all_gather | solution.py:98
  409.4 17.5 %collective-permute-start.3 = (f32[256,256]{0,1:T(8,128)S(1)}, f32[256,256]{0,1:T(8,128)S(1)}, u32[]{:S(2)}, u32[]{:S(2)}) collective-permute-start(f32[256,256]{0,1:T(8,128)S(1)} %copy.61), channel_id=1, source_target_pairs={{0,4},{4,8},{8,12},{12,16},{16,20},{20,24},{24,28},{1,5},{5,9},{9,... | collective-permute-start | bytes 786440 | tf_op jit(solution)/shard_map/ppermute | solution.py:12
  428.2 9.3 collective-permute-done.3
  437.6 7.4 all-gather.4
  446.5 5.0 collective-permute-start.5
  454.0 7.0 all_gather.78
  463.3 5.0 conditional.9
  474.3 14.1 %all-to-all-done.2 = f32[2,512,256]{2,1,0:T(8,128)S(1)} async-done(((f32[2,512,256]{2,1,0:T(8,128)}), f32[2,512,256]{2,1,0:T(8,128)S(1)}, u32[]{:S(2)}, u32[]{:S(2)}) %all-to-all-start.2) | async-done | bytes 1048608 | tf_op jit(solution)/shard_map/all_to_all | solution.py:96
  488.4 159.4 %all-gather.26.cloned.1.call-done = f32[512,512]{1,0:T(8,128)} async-done(((f32[512,256]{1,0:T(8,128)}), f32[512,512]{1,0:T(8,128)}) %all-gather.26.cloned.1.call-update) | async-done | bytes 1048592 | tf_op jit(solution)/shard_map/all_gather | solution.py:98
  648.2 18.6 %collective-permute-start.7 = (f32[256,256]{0,1:T(8,128)S(1)}, f32[256,256]{0,1:T(8,128)S(1)}, u32[]{:S(2)}, u32[]{:S(2)}) collective-permute-start(f32[256,256]{0,1:T(8,128)S(1)} %copy.65), channel_id=1, source_target_pairs={{0,8},{4,12},{8,16},{12,20},{16,24},{20,28},{1,9},{5,13},{9,17},{1... | collective-permute-start | bytes 786440 | tf_op jit(solution)/shard_map/ppermute | solution.py:12
  676.7 7.1 all-gather.6
  685.4 4.6 collective-permute-start.9
  692.4 7.0 all_gather.83
  701.7 5.3 conditional.11
  713.0 14.1 %all-to-all-done.3 = f32[2,512,256]{2,1,0:T(8,128)S(1)} async-done(((f32[2,512,256]{2,1,0:T(8,128)}), f32[2,512,256]{2,1,0:T(8,128)S(1)}, u32[]{:S(2)}, u32[]{:S(2)}) %all-to-all-start.3) | async-done | bytes 1048608 | tf_op jit(solution)/shard_map/all_to_all | solution.py:96
  727.1 150.0 %all-gather.28.cloned.1.call-done = f32[512,512]{1,0:T(8,128)} async-done(((f32[512,256]{1,0:T(8,128)}), f32[512,512]{1,0:T(8,128)}) %all-gather.28.cloned.1.call-update) | async-done | bytes 1048592 | tf_op jit(solution)/shard_map/all_gather | solution.py:98
  877.5 20.1 %collective-permute-start.11 = (f32[256,256]{0,1:T(8,128)S(1)}, f32[256,256]{0,1:T(8,128)S(1)}, u32[]{:S(2)}, u32[]{:S(2)}) collective-permute-start(f32[256,256]{0,1:T(8,128)S(1)} %copy.69), channel_id=1, source_target_pairs={{0,16},{4,20},{8,24},{12,28},{1,17},{5,21},{9,25},{13,29},{2,18},{... | collective-permute-start | bytes 786440 | tf_op jit(solution)/shard_map/ppermute | solution.py:12
  902.5 10.6 collective-permute-done.10
  913.2 7.1 all-gather.8
  922.0 7.8 collective-permute-done.12
  931.9 136.4 %conditional.13 = (f32[128]{0:T(128)S(1)}) conditional(s32[]{:T(128)} %convert_element_type.34, () %tuple.76, (f32[1,512,512]{1,2,0:T(8,128)}, s32[]{:T(128)}) %tuple.256), branch_computations={%region_23.26_spmd, %region_24.28_spmd} | conditional | flops 656916992 | bytes 27548512 | solution.py:146
  935.0 11.7 %cholesky.766 = f32[128,128]{1,0:T(8,128)S(1)} custom-call(f32[128,128]{1,0:T(8,128)S(1)} %cholesky.919), custom_call_target="Cholesky" | custom-call | tf_op jit(solution)/shard_map/cond/branch_1_fun/jit(cholesky)/cholesky | solution.py:20
  946.8 9.8 custom-call.54
  957.4 11.7 %cholesky.785 = f32[128,128]{1,0:T(8,128)S(1)} custom-call(f32[128,128]{1,0:T(8,128)S(1)} %cholesky.923), custom_call_target="Cholesky" | custom-call | tf_op jit(solution)/shard_map/cond/branch_1_fun/jit(cholesky)/cholesky | solution.py:20
  971.1 10.0 custom-call.55
  981.8 11.7 %cholesky.806 = f32[128,128]{1,0:T(8,128)S(1)} custom-call(f32[128,128]{1,0:T(8,128)S(1)} %cholesky.928), custom_call_target="Cholesky" | custom-call | tf_op jit(solution)/shard_map/cond/branch_1_fun/jit(cholesky)/cholesky | solution.py:20
  994.8 9.8 custom-call.56
  1005.2 11.7 %cholesky.823 = f32[128,128]{1,0:T(8,128)S(1)} custom-call(f32[128,128]{1,0:T(8,128)S(1)} %convolution_subtract_fusion.11), custom_call_target="Cholesky" | custom-call | tf_op jit(solution)/shard_map/cond/branch_1_fun/jit(cholesky)/cholesky | solution.py:20
  1018.5 8.1 while.12
  1026.6 39.3 %custom-call.26 = f32[4,128,128]{1,2,0:T(8,128)S(1)} custom-call(f32[4,128,128]{2,1,0:T(8,128)S(1)} %get-tuple-element.144), custom_call_target="InvertDiagBlocksLowerTriangular" | custom-call | tf_op jit(solution)/shard_map/cond/branch_1_fun/jit(_solve_triangular)/triangular_solve | solution.py:21
  (255 shorter events, 130.0 us)
Async XLA Ops:
  7.2 12.1 %copy-start.36 = (f32[2,256,256]{2,1,0:T(8,128)S(1)}, f32[2,256,256]{2,1,0:T(8,128)}, u32[]{:S(2)}) copy-start(f32[2,256,256]{2,1,0:T(8,128)} %param.20) | copy-start | bytes 1572868
  7.2 23.8 %all-gather.20.cloned.1.call-start = ((), (), s32[]{:S(2)}) async-start(), calls=%async_computation.4 | async-start | bytes 1572864 | tf_op jit(solution)/shard_map/all_gather | solution.py:42
  9.2 10.3 copy-start.19
  19.2 173.7 %all-gather.22.cloned.1.call-start = ((), (), s32[]{:S(2)}) async-start(), calls=%async_computation.5 | async-start | bytes 1572864 | tf_op jit(solution)/shard_map/all_gather | solution.py:98
  21.8 9.2 copy-start.13
  31.0 2.7 copy-start.6
  178.9 2.5 copy-start
  183.3 18.8 %all-to-all-start = ((f32[2,512,256]{2,1,0:T(8,128)}), f32[2,512,256]{2,1,0:T(8,128)S(1)}, u32[]{:S(2)}, u32[]{:S(2)}) async-start(f32[2,512,256]{2,1,0:T(8,128)} %pad_maximum_fusion.17), calls=%async_computation | async-start | bytes 2097152 | tf_op jit(solution)/shard_map/all_to_all | solution.py:96
  186.9 44.4 %all-gather.30.cloned.1.call-start = ((), (), s32[]{:S(2)}) async-start(), calls=%async_computation.9 | async-start | bytes 1572864 | tf_op jit(solution)/shard_map/all_gather | solution.py:42
  196.0 9.8 collective-permute-start
  207.8 8.5 copy-start.17
  216.3 192.8 %all-gather.24.cloned.1.call-start = ((), (), s32[]{:S(2)}) async-start(), calls=%async_computation.6 | async-start | bytes 1572864 | tf_op jit(solution)/shard_map/all_gather | solution.py:98
  217.3 14.0 %copy-start.15 = (f32[256,256]{0,1:T(8,128)}, f32[256,256]{0,1:T(8,128)S(1)}, u32[]{:S(2)}) copy-start(f32[256,256]{0,1:T(8,128)S(1)} %convolution_negate_fusion.3) | copy-start | bytes 786436
  217.3 11.8 %collective-permute-start.1 = (f32[256,256]{0,1:T(8,128)S(1)}, f32[256,256]{0,1:T(8,128)S(1)}, u32[]{:S(2)}, u32[]{:S(2)}) collective-permute-start(f32[256,256]{0,1:T(8,128)S(1)} %convolution_negate_fusion.3), channel_id=1, source_target_pairs={{0,4},{4,8},{8,12},{12,16},{16,20},{20,24},{24,28},{1,5},{5,9},{9,... | collective-permute-start | bytes 786440 | tf_op jit(solution)/shard_map/ppermute | solution.py:12
  238.7 17.7 %all-to-all-start.1 = ((f32[2,512,256]{2,1,0:T(8,128)}), f32[2,512,256]{2,1,0:T(8,128)S(1)}, u32[]{:S(2)}, u32[]{:S(2)}) async-start(f32[2,512,256]{2,1,0:T(8,128)} %pad_maximum_fusion.18), calls=%async_computation.1 | async-start | bytes 2097152 | tf_op jit(solution)/shard_map/all_to_all | solution.py:96
  242.3 221.0 %all-gather.32.cloned.1.call-start = ((), (), s32[]{:S(2)}) async-start(), calls=%async_computation.10 | async-start | bytes 1572864 | tf_op jit(solution)/shard_map/all_gather | solution.py:42
  409.0 28.5 %copy-start.18 = (f32[256,256]{0,1:T(8,128)S(1)}, f32[256,256]{0,1:T(8,128)}, u32[]{:S(2)}) copy-start(f32[256,256]{0,1:T(8,128)} %copy-done.17) | copy-start | bytes 786436
  409.4 44.6 %copy-start.16 = (f32[256,256]{0,1:T(8,128)S(1)}, f32[256,256]{0,1:T(8,128)}, u32[]{:S(2)}) copy-start(f32[256,256]{0,1:T(8,128)} %copy-done.15) | copy-start | bytes 786436
  409.4 28.1 %collective-permute-start.3 = (f32[256,256]{0,1:T(8,128)S(1)}, f32[256,256]{0,1:T(8,128)S(1)}, u32[]{:S(2)}, u32[]{:S(2)}) collective-permute-start(f32[256,256]{0,1:T(8,128)S(1)} %copy.61), channel_id=1, source_target_pairs={{0,4},{4,8},{8,12},{12,16},{16,20},{20,24},{24,28},{1,5},{5,9},{9,... | collective-permute-start | bytes 786440 | tf_op jit(solution)/shard_map/ppermute | solution.py:12
  426.9 10.6 collective-permute-start.2
  437.6 14.0 %copy-start.25 = (f32[256,256]{0,1:T(8,128)}, f32[256,256]{0,1:T(8,128)S(1)}, u32[]{:S(2)}) copy-start(f32[256,256]{0,1:T(8,128)S(1)} %subtract_subtract_fusion.2) | copy-start | bytes 786436
  445.0 202.8 %all-gather.26.cloned.1.call-start = ((), (), s32[]{:S(2)}) async-start(), calls=%async_computation.7 | async-start | bytes 1572864 | tf_op jit(solution)/shard_map/all_gather | solution.py:98
  445.2 8.7 collective-permute-start.4
  446.5 14.5 %collective-permute-start.5 = (f32[256,256]{1,0:T(8,128)S(1)}, f32[256,256]{1,0:T(8,128)S(1)}, u32[]{:S(2)}, u32[]{:S(2)}) collective-permute-start(f32[256,256]{1,0:T(8,128)S(1)} %get-tuple-element.115), channel_id=1, source_target_pairs={{0,4},{4,8},{8,12},{12,16},{16,20},{20,24},{24,28},{1,5},{5,9},{9,... | collective-permute-start | bytes 786440 | tf_op jit(solution)/shard_map/ppermute | solution.py:12
  454.0 9.4 copy-start.23
  470.7 17.7 %all-to-all-start.2 = ((f32[2,512,256]{2,1,0:T(8,128)}), f32[2,512,256]{2,1,0:T(8,128)S(1)}, u32[]{:S(2)}, u32[]{:S(2)}) async-start(f32[2,512,256]{2,1,0:T(8,128)} %pad_maximum_fusion.19), calls=%async_computation.2 | async-start | bytes 2097152 | tf_op jit(solution)/shard_map/all_to_all | solution.py:96
  474.3 227.4 %all-gather.34.cloned.1.call-start = ((), (), s32[]{:S(2)}) async-start(), calls=%async_computation.11 | async-start | bytes 1572864 | tf_op jit(solution)/shard_map/all_gather | solution.py:42
  647.9 28.1 %copy-start.26 = (f32[256,256]{0,1:T(8,128)S(1)}, f32[256,256]{0,1:T(8,128)}, u32[]{:S(2)}) copy-start(f32[256,256]{0,1:T(8,128)} %copy-done.25) | copy-start | bytes 786436
  648.2 35.7 %copy-start.33 = (f32[256,256]{1,0:T(8,128)S(1)}, f32[256,256]{1,0:T(8,128)}, u32[]{:S(2)}) copy-start(f32[256,256]{1,0:T(8,128)} %copy-done.32) | copy-start | bytes 786436
  648.2 44.1 %copy-start.24 = (f32[256,256]{0,1:T(8,128)S(1)}, f32[256,256]{0,1:T(8,128)}, u32[]{:S(2)}) copy-start(f32[256,256]{0,1:T(8,128)} %copy-done.23) | copy-start | bytes 786436
  648.2 23.6 %collective-permute-start.7 = (f32[256,256]{0,1:T(8,128)S(1)}, f32[256,256]{0,1:T(8,128)S(1)}, u32[]{:S(2)}, u32[]{:S(2)}) collective-permute-start(f32[256,256]{0,1:T(8,128)S(1)} %copy.65), channel_id=1, source_target_pairs={{0,8},{4,12},{8,16},{12,20},{16,24},{20,28},{1,9},{5,13},{9,17},{1... | collective-permute-start | bytes 786440 | tf_op jit(solution)/shard_map/ppermute | solution.py:12
  666.8 9.1 collective-permute-start.6
  683.8 193.3 %all-gather.28.cloned.1.call-start = ((), (), s32[]{:S(2)}) async-start(), calls=%async_computation.8 | async-start | bytes 1572864 | tf_op jit(solution)/shard_map/all_gather | solution.py:98
  684.0 8.3 collective-permute-start.8
  685.4 14.0 %collective-permute-start.9 = (f32[256,256]{1,0:T(8,128)S(1)}, f32[256,256]{1,0:T(8,128)S(1)}, u32[]{:S(2)}, u32[]{:S(2)}) collective-permute-start(f32[256,256]{1,0:T(8,128)S(1)} %copy-done.33), channel_id=1, source_target_pairs={{0,8},{4,12},{8,16},{12,20},{16,24},{20,28},{1,9},{5,13},{9,17},{1... | collective-permute-start | bytes 786440 | tf_op jit(solution)/shard_map/ppermute | solution.py:12
  692.3 9.4 copy-start.27
  709.4 17.7 %all-to-all-start.3 = ((f32[2,512,256]{2,1,0:T(8,128)}), f32[2,512,256]{2,1,0:T(8,128)S(1)}, u32[]{:S(2)}, u32[]{:S(2)}) async-start(f32[2,512,256]{2,1,0:T(8,128)} %pad_maximum_fusion.20), calls=%async_computation.3 | async-start | bytes 2097152 | tf_op jit(solution)/shard_map/all_to_all | solution.py:96
  713.0 218.9 %all-gather.36.cloned.1.call-start = ((), (), s32[]{:S(2)}) async-start(), calls=%async_computation.12 | async-start | bytes 1572864 | tf_op jit(solution)/shard_map/all_gather | solution.py:42
  877.1 36.1 %copy-start.22 = (f32[256,256]{0,1:T(8,128)S(1)}, f32[256,256]{0,1:T(8,128)}, u32[]{:S(2)}) copy-start(f32[256,256]{0,1:T(8,128)} %copy-done.21) | copy-start | bytes 786436
  877.4 43.0 %copy-start.35 = (f32[256,256]{1,0:T(8,128)S(1)}, f32[256,256]{1,0:T(8,128)}, u32[]{:S(2)}) copy-start(f32[256,256]{1,0:T(8,128)} %copy-done.34) | copy-start | bytes 786436
  877.5 44.4 %copy-start.1 = (f32[128,640]{1,0:T(8,128)S(1)}, f32[128,640]{1,0:T(8,128)}, u32[]{:S(2)}) copy-start(f32[128,640]{1,0:T(8,128)} %copy-done) | copy-start | bytes 983044
  877.5 25.1 %collective-permute-start.11 = (f32[256,256]{0,1:T(8,128)S(1)}, f32[256,256]{0,1:T(8,128)S(1)}, u32[]{:S(2)}, u32[]{:S(2)}) collective-permute-start(f32[256,256]{0,1:T(8,128)S(1)} %copy.69), channel_id=1, source_target_pairs={{0,16},{4,20},{8,24},{12,28},{1,17},{5,21},{9,25},{13,29},{2,18},{... | collective-permute-start | bytes 786440 | tf_op jit(solution)/shard_map/ppermute | solution.py:12
  897.5 15.6 %collective-permute-start.10 = (f32[256,256]{0,1:T(8,128)S(1)}, f32[256,256]{0,1:T(8,128)S(1)}, u32[]{:S(2)}, u32[]{:S(2)}) collective-permute-start(f32[256,256]{0,1:T(8,128)S(1)} %copy.68), channel_id=1, source_target_pairs={{16,0},{20,4},{24,8},{28,12},{17,1},{21,5},{25,9},{29,13},{18,2},{... | collective-permute-start | bytes 786440 | tf_op jit(solution)/shard_map/ppermute | solution.py:12
  920.4 9.4 copy-start.28
  920.4 9.4 copy-start.14
  920.6 9.2 collective-permute-start.12
  922.0 8.8 copy-start.20
  935.0 21.7 %copy-start.11 = (f32[512,512]{1,0:T(8,128)S(1)}, f32[512,512]{1,0:T(8,128)}, u32[]{:S(2)}) copy-start(f32[512,512]{1,0:T(8,128)} %copy-done.10) | copy-start | bytes 3145732 | tf_op jit(solution)/shard_map/cond
  (6 other events, 9.2 us)
Sparse Core Ops, SparseCore 0:
  19.4 10.5 all-gather.19
  182.4 10.5 all-gather.21
  216.4 11.2 all-gather.29
  236.5 172.4 all-gather.23
  445.1 10.5 all-gather.31
  468.5 179.3 all-gather.25
  684.0 7.7 all-gather.33
  707.2 169.8 all-gather.27
  920.5 5.4 all-gather.35
